TPU v7x, 32 devices: a whole 2x2x4 slice. The times are simulated.
32 devices in a mesh: dp: 4 (over z), tensor: 8 (over y, x, core).
Axes of the slice: x: 2, y: 2, z: 4, core: 2. Of those that a mesh axis runs over, the one named last changes fastest.
Arguments:
- layer_input: bfloat16 [16384, 2048], P(('dp', 'tensor')), may hold values from -20 to 20
- gain_attn: float32 [2048], replicated, may hold values from 0.25 to 1.75
- w_query: bfloat16 [2048, 2048], P(None, 'tensor'), may hold values from -0.125 to 0.125
- w_key: bfloat16 [2048, 2048], P(None, 'tensor'), may hold values from -0.125 to 0.125
- w_value: bfloat16 [2048, 2048], P(None, 'tensor'), may hold values from -0.125 to 0.125
- w_out: bfloat16 [2048, 2048], P('tensor'), may hold values from -1 to 1
- gain_mlp: float32 [2048], replicated, may hold values from 0.25 to 1.75
- w_gate: bfloat16 [2048, 8192], P(None, 'tensor'), may hold values from -0.125 to 0.125
- w_up: bfloat16 [2048, 8192], P(None, 'tensor'), may hold values from -0.125 to 0.125
- w_down: bfloat16 [8192, 2048], P('tensor'), may hold values from -0.0625 to 0.0625
- segment_ids: int32 [8, 2048], P('dp'), may hold values from 0 to 31, as said below
- positions: int32 [8, 2048], P('dp'), may hold values from 0 to 2047, as said below
- out_grad: bfloat16 [16384, 2048], P(('dp', 'tensor')), may hold values from -6 to 6
Outputs:
- layer_out: bfloat16 [16384, 2048], P(('dp', 'tensor'))
- input_grad: float32 [16384, 2048], P(('dp', 'tensor'))
- grad_gain_attn: float32 [2048], P('tensor')
- grad_w_query: float32 [2048, 2048], P(None, 'tensor')
- grad_w_key: float32 [2048, 2048], P(None, 'tensor')
- grad_w_value: float32 [2048, 2048], P(None, 'tensor')
- grad_w_out: float32 [2048, 2048], P('tensor')
- grad_gain_mlp: float32 [2048], P('tensor')
- grad_w_gate: float32 [2048, 8192], P(None, 'tensor')
- grad_w_up: float32 [2048, 8192], P(None, 'tensor')
- grad_w_down: float32 [8192, 2048], P('tensor')
Inputs may be any that keep to these rules, and one draw needn't show every extreme that they name: `segment_ids`: within each row the document number is 0 at the first token and rises by 0 or 1 from one token to the next; a row holds 1 to 32 documents; the first row of the batch is one document and the last row holds 32. `positions`: A position is 0 where a row begins or the document number changes, else one more than the position before.
All inputs are finite; a program needn't handle non-finite values.
Results may differ from a plain program's by a relative error of at most 0.024.
Values may be sent and summed in bfloat16 or wider, within the bound.
A program may use at most 320 MiB of HBM per device.

v0:
```python
import jax
import jax.numpy as jnp
from jax import lax
from jax.sharding import PartitionSpec as P

HD = 64
rope_theta = 130000.0
norm_eps = 1e-05


def rotary_tables(position_list, head_size):
    half_dim = head_size // 2
    frequency = rope_theta ** (-(jnp.arange(half_dim, dtype=jnp.float32) * 2.0 / head_size))
    angles = position_list.astype(jnp.float32)[:, None] * frequency[None, :]
    cosine_table = jnp.concatenate([jnp.cos(angles), jnp.cos(angles)], axis=-1)[:, None, :]
    sine_table = jnp.concatenate([jnp.sin(angles), jnp.sin(angles)], axis=-1)[:, None, :]
    return (cosine_table, sine_table)


def rotate(inputs, cosine_table, sine_table):
    half_dim = inputs.shape[-1] // 2
    turned = jnp.concatenate([-inputs[..., half_dim:], inputs[..., :half_dim]], axis=-1)
    return inputs * cosine_table + turned * sine_table


def rotate_back(grad_in, cosine_table, sine_table):
    half_dim = grad_in.shape[-1] // 2
    scaled = grad_in * sine_table
    turned = jnp.concatenate([scaled[..., half_dim:], -scaled[..., :half_dim]], axis=-1)
    return grad_in * cosine_table + turned


def normalize(row_values):
    inverse = lax.rsqrt(jnp.mean(row_values * row_values, axis=-1, keepdims=True) + norm_eps)
    return (row_values * inverse, inverse)


def norm_back(grad_in, gain_vec, unit_rows, inverse):
    scaled = grad_in * gain_vec
    return inverse * (scaled - unit_rows * jnp.mean(scaled * unit_rows, axis=-1, keepdims=True))


def project_attend(gathered, joined_w, position_ids, hidden_w):
    token_count = gathered.shape[0]
    local_heads = hidden_w // HD
    projected = jnp.dot(gathered, joined_w, preferred_element_type=jnp.float32)
    cosine_table, sine_table = rotary_tables(position_ids.reshape(-1), HD)
    queries = rotate(
        projected[:, :hidden_w].reshape(token_count, local_heads, HD), cosine_table, sine_table
    ).astype(jnp.bfloat16)
    key_heads = rotate(
        projected[:, hidden_w : 2 * hidden_w].reshape(token_count, local_heads, HD),
        cosine_table,
        sine_table,
    ).astype(jnp.bfloat16)
    value_heads = (
        projected[:, 2 * hidden_w :].reshape(token_count, local_heads, HD).astype(jnp.bfloat16)
    )
    return (queries, key_heads, value_heads, cosine_table, sine_table)


def block_mask(segment_row, first_row, block_len):
    q_index = first_row + jnp.arange(block_len, dtype=jnp.int32)
    k_index = jnp.arange(segment_row.shape[0], dtype=jnp.int32)
    seg_query = lax.dynamic_slice_in_dim(segment_row, first_row, block_len)
    return (seg_query[:, None] == segment_row[None, :]) & (k_index[None, :] <= q_index[:, None])


def block_scores(query_block, key_row, allowed):
    scores = jnp.einsum(
        "qhd,khd->hqk", query_block, key_row, preferred_element_type=jnp.float32
    ) * HD ** (-0.5)
    return jnp.where(allowed[None], scores, -1e30)


def attend_forward(queries, key_heads, value_heads, segment_ids):
    row_count, length = segment_ids.shape
    local_heads = queries.shape[1]
    block_len = min(512, length)
    per_row = length // block_len
    query_rows = queries.reshape(row_count, length, local_heads, HD)
    key_rows = key_heads.reshape(row_count, length, local_heads, HD)
    value_rows = value_heads.reshape(row_count, length, local_heads, HD)

    def one_block(block_index):
        row_index = block_index // per_row
        first_row = block_index % per_row * block_len
        query_block = lax.dynamic_slice_in_dim(query_rows[row_index], first_row, block_len, 0)
        scores = block_scores(
            query_block,
            key_rows[row_index],
            block_mask(segment_ids[row_index], first_row, block_len),
        )
        row_max = jnp.max(scores, axis=-1, keepdims=True)
        exp_scores = jnp.exp(scores - row_max)
        exp_total = jnp.sum(exp_scores, axis=-1, keepdims=True)
        probabilities = (exp_scores / exp_total).astype(jnp.bfloat16)
        mixed = jnp.einsum(
            "hqk,khd->qhd", probabilities, value_rows[row_index], preferred_element_type=jnp.float32
        )
        return (mixed.astype(jnp.bfloat16), (row_max + jnp.log(exp_total))[..., 0])

    mixed_all, log_total = lax.map(one_block, jnp.arange(row_count * per_row, dtype=jnp.int32))
    return (mixed_all.reshape(row_count * length, local_heads * HD), log_total)


def attend_backward(queries, key_heads, value_heads, d_mixed, log_total, segment_ids):
    row_count, length = segment_ids.shape
    local_heads = queries.shape[1]
    block_len = min(512, length)
    per_row = length // block_len
    scale_factor = HD ** (-0.5)
    query_rows = queries.reshape(row_count, length, local_heads, HD)
    key_rows = key_heads.reshape(row_count, length, local_heads, HD)
    value_rows = value_heads.reshape(row_count, length, local_heads, HD)
    grad_rows = d_mixed.reshape(row_count, length, local_heads, HD)

    def one_row(row_index):
        query_row = query_rows[row_index]
        key_row = key_rows[row_index]
        value_row = value_rows[row_index]
        grad_row = grad_rows[row_index]
        segment_row = segment_ids[row_index]

        def one_step(running, block_number):
            d_key_acc, d_value_acc = running
            first_row = block_number * block_len
            query_block = lax.dynamic_slice_in_dim(query_row, first_row, block_len, 0)
            grad_block = lax.dynamic_slice_in_dim(grad_row, first_row, block_len, 0)
            scores = block_scores(
                query_block, key_row, block_mask(segment_row, first_row, block_len)
            )
            level_block = log_total[row_index * per_row + block_number][:, :, None]
            probabilities = jnp.exp(scores - level_block)
            d_probs = jnp.einsum(
                "qhd,khd->hqk", grad_block, value_row, preferred_element_type=jnp.float32
            )
            centre = jnp.sum(d_probs * probabilities, axis=-1, keepdims=True)
            d_scores = (probabilities * (d_probs - centre)).astype(jnp.bfloat16)
            d_query_block = (
                jnp.einsum("hqk,khd->qhd", d_scores, key_row, preferred_element_type=jnp.float32)
                * scale_factor
            )
            d_key_acc = (
                d_key_acc
                + jnp.einsum(
                    "hqk,qhd->khd", d_scores, query_block, preferred_element_type=jnp.float32
                )
                * scale_factor
            )
            d_value_acc = d_value_acc + jnp.einsum(
                "hqk,qhd->khd",
                probabilities.astype(jnp.bfloat16),
                grad_block,
                preferred_element_type=jnp.float32,
            )
            return ((d_key_acc, d_value_acc), d_query_block)

        zero_rows = jnp.zeros((length, local_heads, HD), jnp.float32)
        (d_key_row, d_value_row), d_query_blocks = lax.scan(
            one_step, (zero_rows, zero_rows), jnp.arange(per_row, dtype=jnp.int32)
        )
        return (d_query_blocks.reshape(length, local_heads, HD), d_key_row, d_value_row)

    d_queries, d_keys, d_values = lax.map(one_row, jnp.arange(row_count, dtype=jnp.int32))
    token_count = row_count * length
    return (
        d_queries.reshape(token_count, local_heads, HD),
        d_keys.reshape(token_count, local_heads, HD),
        d_values.reshape(token_count, local_heads, HD),
    )


def mlp_hidden(gathered, both_w, ff_local):
    projected = jnp.dot(gathered, both_w, preferred_element_type=jnp.float32)
    gate_pre = projected[:, :ff_local]
    up_pre = projected[:, ff_local:]
    hidden = (jax.nn.silu(gate_pre) * up_pre).astype(jnp.bfloat16)
    return (gate_pre, up_pre, hidden)


def local(
    layer_input,
    gain_attn,
    w_query,
    w_key,
    w_value,
    w_out,
    gain_mlp,
    w_gate,
    w_up,
    w_down,
    segment_ids,
    positions,
    out_grad,
):
    shard_rows, width = layer_input.shape
    tensor_size = lax.axis_size("tensor")
    hidden_w = w_query.shape[1]
    ff_local = w_gate.shape[1]
    joined_w = jnp.concatenate([w_query, w_key, w_value], axis=1)
    both_w = jnp.concatenate([w_gate, w_up], axis=1)
    inputs = layer_input.astype(jnp.float32)
    unit_one, inverse_one = normalize(inputs)
    normed_one = (unit_one * gain_attn).astype(jnp.bfloat16)
    gathered_one = lax.all_gather(normed_one, "tensor", axis=0, tiled=True)
    queries, key_heads, value_heads, cosine_table, sine_table = project_attend(
        gathered_one, joined_w, positions, hidden_w
    )
    attended, log_total = attend_forward(queries, key_heads, value_heads, segment_ids)
    residual = inputs + lax.psum_scatter(
        jnp.dot(attended, w_out, preferred_element_type=jnp.float32).astype(jnp.bfloat16),
        "tensor",
        scatter_dimension=0,
        tiled=True,
    ).astype(jnp.float32)
    unit_two, inverse_two = normalize(residual)
    normed_two = (unit_two * gain_mlp).astype(jnp.bfloat16)
    gathered_two = lax.all_gather(normed_two, "tensor", axis=0, tiled=True)
    gate_pre, up_pre, hidden = mlp_hidden(gathered_two, both_w, ff_local)
    layer_out = (
        residual
        + lax.psum_scatter(
            jnp.dot(hidden, w_down, preferred_element_type=jnp.float32).astype(jnp.bfloat16),
            "tensor",
            scatter_dimension=0,
            tiled=True,
        ).astype(jnp.float32)
    ).astype(jnp.bfloat16)
    token_count = gathered_two.shape[0]
    shard_piece = lax.all_gather(out_grad, "tensor", axis=0, tiled=True)
    d_down = lax.dot_general(
        hidden, shard_piece, (((0,), (0,)), ((), ())), preferred_element_type=jnp.float32
    )
    part_rows = lax.dot_general(
        shard_piece, w_down, (((1,), (1,)), ((), ())), preferred_element_type=jnp.float32
    )
    d_hidden = part_rows
    sigmoid_gate = jax.nn.sigmoid(gate_pre)
    d_up = d_hidden * (gate_pre * sigmoid_gate)
    d_gate = d_hidden * up_pre * sigmoid_gate * (1.0 + gate_pre * (1.0 - sigmoid_gate))
    d_both = jnp.concatenate([d_gate, d_up], axis=1).astype(jnp.bfloat16)
    grad_both = lax.dot_general(
        gathered_two, d_both, (((0,), (0,)), ((), ())), preferred_element_type=jnp.float32
    )
    rows_here = d_both
    d_normed_two = lax.psum_scatter(
        lax.dot_general(
            rows_here, both_w, (((1,), (1,)), ((), ())), preferred_element_type=jnp.float32
        ).astype(jnp.bfloat16),
        "tensor",
        scatter_dimension=0,
        tiled=True,
    ).astype(jnp.float32)
    gain_two_part = jnp.sum(d_normed_two * unit_two, axis=0)
    d_residual = out_grad.astype(jnp.float32) + norm_back(
        d_normed_two, gain_mlp, unit_two, inverse_two
    )
    d_attn = d_residual.astype(jnp.bfloat16)
    shard_piece = lax.all_gather(d_attn, "tensor", axis=0, tiled=True)
    d_outw = lax.dot_general(
        attended, shard_piece, (((0,), (0,)), ((), ())), preferred_element_type=jnp.float32
    )
    part_rows = lax.dot_general(
        shard_piece, w_out, (((1,), (1,)), ((), ())), preferred_element_type=jnp.float32
    )
    d_queries, d_keys, d_values = attend_backward(
        queries, key_heads, value_heads, part_rows.astype(jnp.bfloat16), log_total, segment_ids
    )
    d_projected = jnp.concatenate(
        [
            rotate_back(d_queries, cosine_table, sine_table).reshape(token_count, hidden_w),
            rotate_back(d_keys, cosine_table, sine_table).reshape(token_count, hidden_w),
            d_values.reshape(token_count, hidden_w),
        ],
        axis=1,
    ).astype(jnp.bfloat16)
    grad_joined = lax.dot_general(
        gathered_one, d_projected, (((0,), (0,)), ((), ())), preferred_element_type=jnp.float32
    )
    rows_here = d_projected
    d_normed_one = lax.psum_scatter(
        lax.dot_general(
            rows_here, joined_w, (((1,), (1,)), ((), ())), preferred_element_type=jnp.float32
        ).astype(jnp.bfloat16),
        "tensor",
        scatter_dimension=0,
        tiled=True,
    ).astype(jnp.float32)
    gain_one_part = jnp.sum(d_normed_one * unit_one, axis=0)
    input_grad = d_residual + norm_back(d_normed_one, gain_attn, unit_one, inverse_one)
    summed_joined, summed_outw, summed_both, summed_down = (
        lax.psum(grad_joined.astype(jnp.bfloat16), "dp").astype(jnp.float32),
        lax.psum(d_outw.astype(jnp.bfloat16), "dp").astype(jnp.float32),
        lax.psum(grad_both.astype(jnp.bfloat16), "dp").astype(jnp.float32),
        lax.psum(d_down.astype(jnp.bfloat16), "dp").astype(jnp.float32),
    )
    gain_one_all, gain_two_all = lax.psum((gain_one_part, gain_two_part), ("dp", "tensor"))
    gain_piece = width // tensor_size
    gain_start = lax.axis_index("tensor") * gain_piece
    grad_gain_one = lax.dynamic_slice_in_dim(gain_one_all, gain_start, gain_piece)
    grad_gain_two = lax.dynamic_slice_in_dim(gain_two_all, gain_start, gain_piece)
    return (
        layer_out,
        input_grad,
        grad_gain_one,
        summed_joined[:, :hidden_w],
        summed_joined[:, hidden_w : 2 * hidden_w],
        summed_joined[:, 2 * hidden_w :],
        summed_outw,
        grad_gain_two,
        summed_both[:, :ff_local],
        summed_both[:, ff_local:],
        summed_down,
    )


def solution(mesh):
    return jax.shard_map(
        local,
        mesh=mesh,
        in_specs=(
            P(("dp", "tensor"), None),
            P(),
            P(None, "tensor"),
            P(None, "tensor"),
            P(None, "tensor"),
            P("tensor", None),
            P(),
            P(None, "tensor"),
            P(None, "tensor"),
            P("tensor", None),
            P("dp", None),
            P("dp", None),
            P(("dp", "tensor"), None),
        ),
        out_specs=(
            P(("dp", "tensor"), None),
            P(("dp", "tensor"), None),
            P("tensor"),
            P(None, "tensor"),
            P(None, "tensor"),
            P(None, "tensor"),
            P("tensor", None),
            P("tensor"),
            P(None, "tensor"),
            P(None, "tensor"),
            P("tensor", None),
        ),
        check_vma=False,
    )
```

profile of v0, /device:TPU:0, one launch (start us, length us, event | category | flops | bytes accessed | tf_op | source)
XLA Modules:
  0.0 2408.1 jit_solution(8862629533431668547)
XLA Ops:
  27.1 79.2 %all-gather.5.cloned.1.call-done = bf16[4096,2048]{1,0:T(8,128)(2,1)} async-done(((bf16[512,2048]{1,0:T(8,128)(2,1)}), bf16[4096,2048]{1,0:T(8,128)(2,1)}) %all-gather.5.cloned.1.call-update) | async-done | bytes 16777232 | tf_op jit(solution)/shard_map/all_gather | solution.py:206
  106.2 20.4 fusion.84
  194.7 164.5 %while.46 = (s32[]{:T(128)}, bf16[8,512,4,64]{1,3,2,0:T(8,128)(2,1)}, f32[8,4,512]{2,1,0:T(4,128)}, s32[8]{0:T(128)S(1)}, bf16[2,2048,4,64]{1,3,2,0:T(8,128)(2,1...) while((s32[]{:T(128)}, ...), condition=%wide.region_4.5_spmd, body=%wide.region_1.4_spmd.sunk | while | flops 1127348736 | bytes 57248256 | solution.py:103
  375.3 115.8 %reduce-scatter.5.cloned.1.call-done = bf16[512,2048]{1,0:T(8,128)(2,1)} async-done(((bf16[4096,2048]{1,0:T(8,128)(2,1)}), bf16[512,2048]{1,0:T(8,128)(2,1)}) %reduce-scatter.5.cloned.1.call-update) | async-done | bytes 2097168 | tf_op jit(solution)/shard_map/reduce_scatter | solution.py:211
  504.8 81.7 %all-gather.7.cloned.1.call-done = bf16[4096,2048]{1,0:T(8,128)(2,1)} async-done(((bf16[512,2048]{1,0:T(8,128)(2,1)}), bf16[4096,2048]{1,0:T(8,128)(2,1)}) %all-gather.7.cloned.1.call-update) | async-done | bytes 16777232 | tf_op jit(solution)/shard_map/all_gather | solution.py:219
  586.5 44.9 %fusion.85 = f32[4096,2048]{0,1:T(8,128)} fusion(bf16[4096,2048]{1,0:T(8,128)(2,1)} %all-gather.7.cloned.1.call-done, bf16[2048,2048]{1,0:T(8,128)(2,1)} %constant_dynamic-update-slice_fusion.3), kind=kOutput, calls=%fused_computation.157 | convolution fusion | flops 34359738368 | bytes 58720256 | tf_op jit(solution)/shard_map/dot_general | solution.py:175
  631.4 46.6 %all-gather.9.cloned.1.call-done = bf16[4096,2048]{1,0:T(8,128)(2,1)} async-done(((bf16[512,2048]{1,0:T(8,128)(2,1)}), bf16[4096,2048]{1,0:T(8,128)(2,1)}) %all-gather.9.cloned.1.call-update) | async-done | bytes 16777232 | tf_op jit(solution)/shard_map/all_gather | solution.py:231
  678.0 36.1 %multiply_convert_fusion.2 = (bf16[4096,1024]{0,1:T(8,128)(2,1)}, bf16[4096,1024]{0,1:T(8,128)(2,1)}, bf16[4096,1024]{0,1:T(8,128)(2,1)}) fusion(f32[4096,2048]{0,1:T(8,128)} %fusion.85, bf16[4096,2048]{1,0:T(8,128)(2,1)} %all-gather.9.cloned.1.call-done, bf16[1024,2048]{1,0:T(8,128)(2,1)} %param.28), kind=kOutput, calls=%fused_computation.64 | convolution fusion | flops 17242783744 | bytes 79691776 | tf_op jit(solution)/shard_map/dot_general | solution.py:235
  714.1 42.1 %convolution_convert_fusion.3 = bf16[4096,2048]{1,0:T(8,128)(2,1)} fusion(bf16[2048,2048]{1,0:T(8,128)(2,1)} %constant_dynamic-update-slice_fusion.3, bf16[4096,1024]{0,1:T(8,128)(2,1)} %get-tuple-element.527, bf16[4096,1024]{0,1:T(8,128)(2,1)} %get-tuple-element.526), kind=kOutput, calls=%fused_computation.71 | convolution fusion | flops 34401681408 | bytes 41943040 | tf_op jit(solution)/shard_map/dot_general | solution.py:248
  756.5 116.1 %reduce-scatter.9.cloned.1.call-done = bf16[512,2048]{1,0:T(8,128)(2,1)} async-done(((bf16[4096,2048]{1,0:T(8,128)(2,1)}), bf16[512,2048]{1,0:T(8,128)(2,1)}) %reduce-scatter.9.cloned.1.call-update) | async-done | bytes 2097168 | tf_op jit(solution)/shard_map/reduce_scatter | solution.py:247
  885.0 24.7 %convolution_convert_fusion.5 = bf16[1024,2048]{1,0:T(8,128)(2,1)} fusion(bf16[4096,1024]{0,1:T(8,128)(2,1)} %get-tuple-element.528, bf16[4096,2048]{1,0:T(8,128)(2,1)} %all-gather.9.cloned.1.call-done), kind=kOutput, calls=%fused_computation.117 | convolution fusion | flops 17181966336 | bytes 29360128 | tf_op jit(solution)/shard_map/dot_general | solution.py:232
  909.7 45.5 %fusion.47 = bf16[2048,2048]{1,0:T(8,128)(2,1)} fusion(bf16[4096,2048]{1,0:T(8,128)(2,1)} %all-gather.7.cloned.1.call-done, bf16[4096,1024]{0,1:T(8,128)(2,1)} %get-tuple-element.527, bf16[4096,1024]{0,1:T(8,128)(2,1)} %get-tuple-element.526), kind=kOutput, calls=%fused_computation.73 | convolution fusion | flops 34397487104 | bytes 41943040 | tf_op jit(solution)/shard_map/dot_general | solution.py:243
  988.5 508.7 %while.48 = (s32[]{:T(128)}, f32[2,2048,4,64]{3,2,1,0:T(4,128)}, f32[2,2048,4,64]{1,0,3,2:T(2,128)}, bf16[2,2048,4,64]{1,3,2,0:T(8,128)(2,1)}, s32[2]{0:T(128)S(...) while((s32[]{:T(128)}, f32[2,2048,4,64]{3,2,1,0:T(4,128)}, ...), condition=%wide.region_14.15_spmd, body=%wide.region_10.14_spmd.sunk | while | flops 2753165824 | bytes 271215808 | solution.py:165
  997.2 195.8 %while.49 = (s32[]{:T(128)}, f32[2048,4,64]{0,2,1:T(8,128)}, f32[2048,4,64]{0,2,1:T(8,128)}, f32[4,512,4,64]{1,3,2,0:T(8,128)}, s32[4]{0:T(128)S(1)}, /*index=5*...) while((s32[]{:T(128)}, f32[2048,4,64]{0,2,1:T(8,128)}, ...), condition=%wide.region_13.13_spmd.clone, body=%wide.region_11.12_spmd.clone.sunk | while | flops 2753165824 | bytes 197798400 | solution.py:160
  1196.7 35.8 %dynamic_update_slice.48 = f32[2,2048,4,64]{1,0,3,2:T(2,128)} dynamic-update-slice(f32[2,2048,4,64]{1,0,3,2:T(2,128)} %get-tuple-element.933, f32[1,2048,4,64]{1,0,3,2:T(1,128)S(1)} %copy.68, s32[]{:T(128)S(6)} %copy.103, s32[]{:T(128)} %constant.248.clone.1..sunk.1, s32[]{:T(128)} %constant.248.clone.1..sunk.1, s32[]{:T(128)} %constant.248.clone.1..sunk.1) | dynamic-update-slice | bytes 4194308 | tf_op jit(solution)/shard_map/while/body/jit(dynamic_update_index_in_dim)/dynamic_update_slice | solution.py:165
  1251.3 195.8 %while.49 = (s32[]{:T(128)}, f32[2048,4,64]{0,2,1:T(8,128)}, f32[2048,4,64]{0,2,1:T(8,128)}, f32[4,512,4,64]{1,3,2,0:T(8,128)}, s32[4]{0:T(128)S(1)}, /*index=5*...) while((s32[]{:T(128)}, f32[2048,4,64]{0,2,1:T(8,128)}, ...), condition=%wide.region_13.13_spmd.clone, body=%wide.region_11.12_spmd.clone.sunk | while | flops 2753165824 | bytes 197798400 | solution.py:160
  1450.8 35.8 %dynamic_update_slice.48 = f32[2,2048,4,64]{1,0,3,2:T(2,128)} dynamic-update-slice(f32[2,2048,4,64]{1,0,3,2:T(2,128)} %get-tuple-element.933, f32[1,2048,4,64]{1,0,3,2:T(1,128)S(1)} %copy.68, s32[]{:T(128)S(6)} %copy.103, s32[]{:T(128)} %constant.248.clone.1..sunk.1, s32[]{:T(128)} %constant.248.clone.1..sunk.1, s32[]{:T(128)} %constant.248.clone.1..sunk.1) | dynamic-update-slice | bytes 4194308 | tf_op jit(solution)/shard_map/while/body/jit(dynamic_update_index_in_dim)/dynamic_update_slice | solution.py:165
  1573.2 18.9 convolution_convert_fusion.6
  1592.1 19.8 convolution_convert_fusion
  1612.1 25.2 %convolution_convert_fusion.1 = bf16[4096,2048]{1,0:T(8,128)(2,1)} fusion(bf16[4096,1024]{0,1:T(8,128)(2,1)} %get-tuple-element.528, bf16[1024,2048]{1,0:T(8,128)(2,1)} %param.28), kind=kOutput, calls=%fused_computation.69 | convolution fusion | flops 17188257792 | bytes 29360128 | tf_op jit(solution)/shard_map/dot_general | solution.py:224
  1637.3 517.2 %all-reduce.4.cloned.1.call-done = (bf16[2048,768]{1,0:T(8,128)(2,1)}, bf16[256,2048]{1,0:T(8,128)(2,1)}, bf16[2048,2048]{1,0:T(8,128)(2,1)}, bf16[1024,2048]{1,0:T(8,128)(2,1)}) async-done(((bf16[2048,768]{1,0:T(8,128)(2,1)}, bf16[256,2048]{1,0:T(8,128)(2,1)}, bf16[2048,2048]{1,0:T(8,128)(2,1)}, bf16[1024,2048]{1,0:T(8,128)(2,1)}), (bf16[2048,768]{1,0:T(8,128)(2,1)}, bf16[256,2048]{1,0:T(8,128)(2,1)}, ...) | async-done | bytes 16777232 | tf_op jit(solution)/shard_map/psum | solution.py:293
  2183.6 89.6 %reduce-scatter.11.cloned.1.call-done = bf16[512,2048]{1,0:T(8,128)(2,1)} async-done(((bf16[4096,2048]{1,0:T(8,128)(2,1)}), bf16[512,2048]{1,0:T(8,128)(2,1)}) %reduce-scatter.11.cloned.1.call-update) | async-done | bytes 2097168 | tf_op jit(solution)/shard_map/reduce_scatter | solution.py:282
  2276.1 39.5 %all-reduce = (f32[2048]{0:T(1024)S(1)}, f32[2048]{0:T(1024)S(1)}) all-reduce(f32[2048]{0:T(1024)S(1)} %get-tuple-element.446, f32[2048]{0:T(1024)S(1)} %copy-done.43), channel_id=1, replica_groups=mesh['dp'=4,'tensor'=8] {'dp','tensor'}, use_global_device_ids=true, to_apply=%region_18.19 | all-reduce | flops 4096 | bytes 32768 | tf_op jit(solution)/shard_map/psum | solution.py:298
  2317.0 76.2 %reduce-scatter.7.cloned.1.call-done = bf16[512,2048]{1,0:T(8,128)(2,1)} async-done(((bf16[4096,2048]{1,0:T(8,128)(2,1)}), bf16[512,2048]{1,0:T(8,128)(2,1)}) %reduce-scatter.7.cloned.1.call-update) | async-done | bytes 2097168 | tf_op jit(solution)/shard_map/reduce_scatter | solution.py:223
  (475 shorter events, 843.9 us)
Async XLA Ops:
  7.2 357.8 %copy-start = (bf16[256,2048]{1,0:T(8,128)(2,1)S(1)}, bf16[256,2048]{1,0:T(8,128)(2,1)}, u32[]{:S(2)}) copy-start(bf16[256,2048]{1,0:T(8,128)(2,1)} %param.24) | copy-start | bytes 3145732
  7.2 99.0 %all-gather.5.cloned.1.call-start = ((), (), s32[]{:S(2)}) async-start(), calls=%async_computation.4 | async-start | bytes 18874368 | tf_op jit(solution)/shard_map/all_gather | solution.py:206
  13.6 477.5 %reduce-scatter.5.cloned.1.call-start = ((), (), s32[]{:S(2)}) async-start(), calls=%async_computation.5 | async-start | bytes 18874368 | tf_op jit(solution)/shard_map/reduce_scatter | solution.py:211
  374.7 116.4 %copy-start.7 = (bf16[512,2048]{1,0:T(8,128)(2,1)S(1)}, bf16[512,2048]{1,0:T(8,128)(2,1)}, u32[]{:S(2)}) copy-start(bf16[512,2048]{1,0:T(8,128)(2,1)} %param.19) | copy-start | bytes 6291460
  374.8 119.5 %copy-start.33 = (f32[2048]{0:T(1024)S(1)}, f32[2048]{0:T(1024)}, u32[]{:S(2)}) copy-start(f32[2048]{0:T(1024)} %param.25) | copy-start | bytes 24580
  374.8 211.7 %all-gather.7.cloned.1.call-start = ((), (), s32[]{:S(2)}) async-start(), calls=%async_computation.6 | async-start | bytes 18874368 | tf_op jit(solution)/shard_map/all_gather | solution.py:219
  496.6 181.4 %all-gather.9.cloned.1.call-start = ((), (), s32[]{:S(2)}) async-start(), calls=%async_computation.8 | async-start | bytes 18874368 | tf_op jit(solution)/shard_map/all_gather | solution.py:231
  497.2 375.4 %reduce-scatter.9.cloned.1.call-start = ((), (), s32[]{:S(2)}) async-start(), calls=%async_computation.9 | async-start | bytes 18874368 | tf_op jit(solution)/shard_map/reduce_scatter | solution.py:247
  756.2 116.4 %copy-start.8 = (bf16[512,2048]{1,0:T(8,128)(2,1)S(1)}, bf16[512,2048]{1,0:T(8,128)(2,1)}, u32[]{:S(2)}) copy-start(bf16[512,2048]{1,0:T(8,128)(2,1)} %param.19) | copy-start | bytes 6291460
  756.2 116.4 %copy-start.34 = (f32[2048]{0:T(1024)S(1)}, f32[2048]{0:T(1024)}, u32[]{:S(2)}) copy-start(f32[2048]{0:T(1024)} %param.25) | copy-start | bytes 24580
  756.2 116.4 %copy-start.39 = (f32[512]{0:T(512)S(1)}, f32[512]{0:T(512)}, u32[]{:S(2)}) copy-start(f32[512]{0:T(512)} %copy-done.38) | copy-start | bytes 6148
  756.2 215.1 %all-gather.11.cloned.1.call-start = ((), (), s32[]{:S(2)}) async-start(), calls=%async_computation.10 | async-start | bytes 18874368 | tf_op jit(solution)/shard_map/all_gather | solution.py:260
  881.5 1273.0 %all-reduce.4.cloned.1.call-start = ((), (), s32[]{:S(2)}) async-start(), calls=%async_computation.12 | async-start | bytes 33554432 | tf_op jit(solution)/shard_map/psum | solution.py:293
  1561.2 12.0 copy-start.26
  1561.2 12.0 copy-start.27
  1592.1 681.1 %reduce-scatter.11.cloned.1.call-start = ((), (), s32[]{:S(2)}) async-start(), calls=%async_computation.11 | async-start | bytes 18874368 | tf_op jit(solution)/shard_map/reduce_scatter | solution.py:282
  1612.0 781.1 %reduce-scatter.7.cloned.1.call-start = ((), (), s32[]{:S(2)}) async-start(), calls=%async_computation.7 | async-start | bytes 18874368 | tf_op jit(solution)/shard_map/reduce_scatter | solution.py:223
  2167.9 105.3 %copy-start.9 = (bf16[512,2048]{1,0:T(8,128)(2,1)S(1)}, bf16[512,2048]{1,0:T(8,128)(2,1)}, u32[]{:S(2)}) copy-start(bf16[512,2048]{1,0:T(8,128)(2,1)} %param.19) | copy-start | bytes 6291460
  2167.9 105.3 %copy-start.36 = (f32[2048]{0:T(1024)S(1)}, f32[2048]{0:T(1024)}, u32[]{:S(2)}) copy-start(f32[2048]{0:T(1024)} %param.20) | copy-start | bytes 24580
  2167.9 105.3 %copy-start.42 = (f32[512]{0:T(512)S(1)}, f32[512]{0:T(512)}, u32[]{:S(2)}) copy-start(f32[512]{0:T(512)} %copy-done.41) | copy-start | bytes 6148
  2183.5 92.6 %copy-start.43 = (f32[2048]{0:T(1024)S(1)}, f32[2048]{0:T(1024)}, u32[]{:S(2)}) copy-start(f32[2048]{0:T(1024)} %get-tuple-element.444) | copy-start | bytes 24580
  2183.6 209.6 %copy-start.35 = (f32[2048]{0:T(1024)S(1)}, f32[2048]{0:T(1024)}, u32[]{:S(2)}) copy-start(f32[2048]{0:T(1024)} %param.25) | copy-start | bytes 24580
  2183.6 209.6 %copy-start.40 = (f32[512]{0:T(512)S(1)}, f32[512]{0:T(512)}, u32[]{:S(2)}) copy-start(f32[512]{0:T(512)} %copy-done.38) | copy-start | bytes 6148
  2183.6 209.6 %copy-start.45 = (f32[512]{0:T(512)S(1)}, f32[512]{0:T(512)}, u32[]{:S(2)}) copy-start(f32[512]{0:T(512)} %copy-done.44) | copy-start | bytes 6148
  (85 other events, 454.8 us)
Sparse Core Ops, SparseCore 0:
  13.8 92.4 all-gather.4
  374.9 116.1 reduce-scatter.4
  496.7 89.7 all-gather.6
  588.2 89.7 all-gather.8
  756.4 116.1 reduce-scatter.8
  881.6 89.7 all-gather.10
  1592.2 562.2 all-reduce.3
  2158.1 115.1 reduce-scatter.10
  2276.8 116.3 reduce-scatter.6
where the time goes:
time: 2430 us; the launch traced here: 2410 us
  waiting for transfers between devices  1140 us (47%)
  matrix products  661 us (27%)
  local copies, waits for them, and re-layouts  296 us (12%)
  other arithmetic  218 us (9%)
  blocking collectives  39.5 us (2%)
  loops' own time  38.3 us (2%)
    psum x1, waiting for transfers between devices, local(): lax.psum(grad_joined.astype(jnp.bfloat16), 'dp').astype(jnp.float32)  517 us
    reduce_scatter x1, waiting for transfers between devices, local(): lax.psum_scatter(lax.dot_general(rows_here, both_w, (((1,), (1,)), ((), (...  116 us
    reduce_scatter x1, waiting for transfers between devices, local(): lax.psum_scatter(jnp.dot(attended, w_out, preferred_element_type=jnp.floa...  116 us
    dot_general x8, matrix products, one_step(): jnp.einsum('qhd,khd->hqk', grad_block, value_row, preferred_element_type=...  91.3 us
    reduce_scatter x1, waiting for transfers between devices, local(): lax.psum_scatter(lax.dot_general(rows_here, joined_w, (((1,), (1,)), ((),...  89.6 us
    dynamic_update_slice x8, local copies, waits for them, and re-layouts, attend_backward(): lax.map(one_row, jnp.arange(row_count, dtype=jnp.int32))  89.2 us
    all_gather x1, waiting for transfers between devices, local(): gathered_two = lax.all_gather(normed_two, 'tensor', axis=0, tiled=True)  81.7 us
    all_gather x1, waiting for transfers between devices, local(): gathered_one = lax.all_gather(normed_one, 'tensor', axis=0, tiled=True)  79.2 us
  transfers between devices with their start and end apart: 9, of which 9 were waited for; matrix products, arithmetic and copies ran while one was open for 9% of the time, Pallas kernels for 0%

commit v1 on v0

--- a/solution.py
+++ b/solution.py
@@ -6,6 +6,10 @@
 HD = 64
 rope_theta = 130000.0
 norm_eps = 1e-05
+
+
+def close_results(w_in):
+    return jnp.sum(lax.all_gather(w_in, "dp"), axis=0)
 
 
 def rotary_tables(position_list, head_size):
@@ -290,7 +294,7 @@
     gain_one_part = jnp.sum(d_normed_one * unit_one, axis=0)
     input_grad = d_residual + norm_back(d_normed_one, gain_attn, unit_one, inverse_one)
     summed_joined, summed_outw, summed_both, summed_down = (
-        lax.psum(grad_joined.astype(jnp.bfloat16), "dp").astype(jnp.float32),
+        close_results(grad_joined.astype(jnp.bfloat16)).astype(jnp.float32),
         lax.psum(d_outw.astype(jnp.bfloat16), "dp").astype(jnp.float32),
         lax.psum(grad_both.astype(jnp.bfloat16), "dp").astype(jnp.float32),
         lax.psum(d_down.astype(jnp.bfloat16), "dp").astype(jnp.float32),

time: 2430 us -> 2190 us (0.901)
  waiting for transfers between devices: 1140 us -> 788 us
  matrix products: 661 us -> 768 us
    psum x1, waiting for transfers between devices: 517 us -> 0.02 us  [local(): lax.psum(d_outw.astype(jnp.bfloat16), 'dp').astype(jnp.float32)]
    all_gather x0 -> x1, waiting for transfers between devices: none -> 153 us  [close_results(): return jnp.sum(lax.all_gather(w_in, 'dp'), axis=0)]
    dot_general x8, matrix products: 60.2 us -> 98.7 us  [one_step(): jnp.einsum('hqk,qhd->khd', probabilities.astype(jnp.bfloat16), grad_block...]
    dot_general x16, matrix products: 71.8 us -> 107 us  [block_scores(): jnp.einsum('qhd,khd->hqk', query_block, key_row, preferred_element_type=j...]
    dot_general x8, matrix products: 91.3 us -> 126 us  [one_step(): jnp.einsum('qhd,khd->hqk', grad_block, value_row, preferred_element_type=...]
    dot_general x8, matrix products: 22.9 us -> 56.4 us  [one_step(): jnp.einsum('hqk,qhd->khd', d_scores, query_block, preferred_element_type=...]
    dot_general x8, matrix products: 61.1 us -> 27.7 us  [one_step(): jnp.einsum('hqk,khd->qhd', d_scores, key_row, preferred_element_type=jnp....]
  transfers between devices with their start and end apart: 9 -> 10, of which waited for: 9 -> 9; matrix products, arithmetic and copies ran while one was open for 9% -> 41% of each run, Pallas kernels for 0% -> 0%
where the time goes in v1:
time: 2190 us; the launch traced here: 2170 us
  waiting for transfers between devices  788 us (36%)
  matrix products  768 us (35%)
  local copies, waits for them, and re-layouts  278 us (13%)
  other arithmetic  241 us (11%)
  blocking collectives  39.5 us (2%)
  loops' own time  38.4 us (2%)
    all_gather x1, waiting for transfers between devices, close_results(): return jnp.sum(lax.all_gather(w_in, 'dp'), axis=0)  153 us
    dot_general x8, matrix products, one_step(): jnp.einsum('qhd,khd->hqk', grad_block, value_row, preferred_element_type=...  126 us
    reduce_scatter x1, waiting for transfers between devices, local(): lax.psum_scatter(lax.dot_general(rows_here, both_w, (((1,), (1,)), ((), (...  116 us
    reduce_scatter x1, waiting for transfers between devices, local(): lax.psum_scatter(jnp.dot(attended, w_out, preferred_element_type=jnp.floa...  116 us
    dot_general x16, matrix products, block_scores(): jnp.einsum('qhd,khd->hqk', query_block, key_row, preferred_element_type=j...  107 us
    reduce_scatter x1, waiting for transfers between devices, local(): lax.psum_scatter(lax.dot_general(rows_here, joined_w, (((1,), (1,)), ((),...  103 us
    dot_general x8, matrix products, one_step(): jnp.einsum('hqk,qhd->khd', probabilities.astype(jnp.bfloat16), grad_block...  98.7 us
    dynamic_update_slice x8, local copies, waits for them, and re-layouts, attend_backward(): lax.map(one_row, jnp.arange(row_count, dtype=jnp.int32))  89.2 us
  transfers between devices with their start and end apart: 10, of which 9 were waited for; matrix products, arithmetic and copies ran while one was open for 41% of the time, Pallas kernels for 0%

profile of v1, /device:TPU:0, one launch (start us, length us, event | category | flops | bytes accessed | tf_op | source)
XLA Modules:
  0.0 2169.0 jit_solution(8127480997387076564)
XLA Ops:
  27.1 79.2 %all-gather.7.cloned.1.call-done = bf16[4096,2048]{1,0:T(8,128)(2,1)} async-done(((bf16[512,2048]{1,0:T(8,128)(2,1)}), bf16[4096,2048]{1,0:T(8,128)(2,1)}) %all-gather.7.cloned.1.call-update) | async-done | bytes 16777232 | tf_op jit(solution)/shard_map/all_gather | solution.py:210
  106.2 20.4 fusion.84
  193.8 163.8 %while.46 = (s32[]{:T(128)}, bf16[8,512,4,64]{1,3,2,0:T(8,128)(2,1)}, f32[8,4,512]{2,1,0:T(4,128)}, s32[8]{0:T(128)S(1)}, bf16[2,2048,4,64]{1,3,2,0:T(8,128)(2,1...) while((s32[]{:T(128)}, ...), condition=%wide.region_4.5_spmd, body=%wide.region_1.4_spmd.sunk | while | flops 1127348736 | bytes 65637900 | solution.py:107
  373.6 115.8 %reduce-scatter.5.cloned.1.call-done = bf16[512,2048]{1,0:T(8,128)(2,1)} async-done(((bf16[4096,2048]{1,0:T(8,128)(2,1)}), bf16[512,2048]{1,0:T(8,128)(2,1)}) %reduce-scatter.5.cloned.1.call-update) | async-done | bytes 2097168 | tf_op jit(solution)/shard_map/reduce_scatter | solution.py:215
  503.0 81.7 %all-gather.9.cloned.1.call-done = bf16[4096,2048]{1,0:T(8,128)(2,1)} async-done(((bf16[512,2048]{1,0:T(8,128)(2,1)}), bf16[4096,2048]{1,0:T(8,128)(2,1)}) %all-gather.9.cloned.1.call-update) | async-done | bytes 16777232 | tf_op jit(solution)/shard_map/all_gather | solution.py:223
  584.8 44.9 %fusion.85 = f32[4096,2048]{0,1:T(8,128)} fusion(bf16[4096,2048]{1,0:T(8,128)(2,1)} %all-gather.9.cloned.1.call-done, bf16[2048,2048]{1,0:T(8,128)(2,1)} %constant_dynamic-update-slice_fusion.3), kind=kOutput, calls=%fused_computation.157 | convolution fusion | flops 34359738368 | bytes 58720256 | tf_op jit(solution)/shard_map/dot_general | solution.py:179
  629.7 46.6 %all-gather.11.cloned.1.call-done = bf16[4096,2048]{1,0:T(8,128)(2,1)} async-done(((bf16[512,2048]{1,0:T(8,128)(2,1)}), bf16[4096,2048]{1,0:T(8,128)(2,1)}) %all-gather.11.cloned.1.call-update) | async-done | bytes 16777232 | tf_op jit(solution)/shard_map/all_gather | solution.py:235
  676.3 36.1 %multiply_convert_fusion.2 = (bf16[4096,1024]{0,1:T(8,128)(2,1)}, bf16[4096,1024]{0,1:T(8,128)(2,1)}, bf16[4096,1024]{0,1:T(8,128)(2,1)}) fusion(f32[4096,2048]{0,1:T(8,128)} %fusion.85, bf16[4096,2048]{1,0:T(8,128)(2,1)} %all-gather.11.cloned.1.call-done, bf16[1024,2048]{1,0:T(8,128)(2,1)} %param.28), kind=kOutput, calls=%fused_computation.64 | convolution fusion | flops 17242783744 | bytes 79691776 | tf_op jit(solution)/shard_map/dot_general | solution.py:239
  712.4 42.1 %convolution_convert_fusion.3 = bf16[4096,2048]{1,0:T(8,128)(2,1)} fusion(bf16[2048,2048]{1,0:T(8,128)(2,1)} %constant_dynamic-update-slice_fusion.3, bf16[4096,1024]{0,1:T(8,128)(2,1)} %get-tuple-element.526, bf16[4096,1024]{0,1:T(8,128)(2,1)} %get-tuple-element.525), kind=kOutput, calls=%fused_computation.71 | convolution fusion | flops 34401681408 | bytes 41943040 | tf_op jit(solution)/shard_map/dot_general | solution.py:252
  755.0 115.9 %reduce-scatter.9.cloned.1.call-done = bf16[512,2048]{1,0:T(8,128)(2,1)} async-done(((bf16[4096,2048]{1,0:T(8,128)(2,1)}), bf16[512,2048]{1,0:T(8,128)(2,1)}) %reduce-scatter.9.cloned.1.call-update) | async-done | bytes 2097168 | tf_op jit(solution)/shard_map/reduce_scatter | solution.py:251
  883.3 24.7 %convolution_convert_fusion.5 = bf16[1024,2048]{1,0:T(8,128)(2,1)} fusion(bf16[4096,1024]{0,1:T(8,128)(2,1)} %get-tuple-element.527, bf16[4096,2048]{1,0:T(8,128)(2,1)} %all-gather.11.cloned.1.call-done), kind=kOutput, calls=%fused_computation.117 | convolution fusion | flops 17181966336 | bytes 29360128 | tf_op jit(solution)/shard_map/dot_general | solution.py:236
  907.9 45.2 %fusion.47 = bf16[2048,2048]{1,0:T(8,128)(2,1)} fusion(bf16[4096,2048]{1,0:T(8,128)(2,1)} %all-gather.9.cloned.1.call-done, bf16[4096,1024]{0,1:T(8,128)(2,1)} %get-tuple-element.526, bf16[4096,1024]{0,1:T(8,128)(2,1)} %get-tuple-element.525), kind=kOutput, calls=%fused_computation.73 | convolution fusion | flops 34397487104 | bytes 41943040 | tf_op jit(solution)/shard_map/dot_general | solution.py:247
  997.6 620.2 %while.48 = (s32[]{:T(128)}, f32[2,2048,4,64]{3,2,1,0:T(4,128)}, f32[2,2048,4,64]{1,0,3,2:T(2,128)}, bf16[2,2048,4,64]{1,3,2,0:T(8,128)(2,1)}, s32[2]{0:T(128)S(...) while((s32[]{:T(128)}, f32[2,2048,4,64]{3,2,1,0:T(4,128)}, ...), condition=%wide.region_14.15_spmd, body=%wide.region_10.14_spmd.sunk | while | flops 2753165824 | bytes 302674656 | solution.py:169
  1006.6 252.4 %while.49 = (s32[]{:T(128)}, f32[2048,4,64]{0,2,1:T(8,128)}, f32[2048,4,64]{0,2,1:T(8,128)}, f32[4,512,4,64]{1,3,2,0:T(8,128)}, s32[4]{0:T(128)S(1)}, /*index=5*...) while((s32[]{:T(128)}, f32[2048,4,64]{0,2,1:T(8,128)}, ...), condition=%wide.region_13.13_spmd.clone, body=%wide.region_11.12_spmd.clone.sunk | while | flops 2753165824 | bytes 243936352 | solution.py:164
  1269.8 35.9 %dynamic_update_slice.48 = f32[2,2048,4,64]{1,0,3,2:T(2,128)} dynamic-update-slice(f32[2,2048,4,64]{1,0,3,2:T(2,128)} %get-tuple-element.932, f32[1,2048,4,64]{1,0,3,2:T(1,128)S(1)} %copy.68, s32[]{:T(128)} %get-tuple-element.930, s32[]{:T(128)} %constant.249.clone.1..sunk.1, s32[]{:T(128)} %constant.249.clone.1..sunk.1, s32[]{:T(128)} %constant.249.clone.1..sunk.1) | dynamic-update-slice | bytes 4194308 | tf_op jit(solution)/shard_map/while/body/jit(dynamic_update_index_in_dim)/dynamic_update_slice | solution.py:169
  1316.7 251.6 %while.49 = (s32[]{:T(128)}, f32[2048,4,64]{0,2,1:T(8,128)}, f32[2048,4,64]{0,2,1:T(8,128)}, f32[4,512,4,64]{1,3,2,0:T(8,128)}, s32[4]{0:T(128)S(1)}, /*index=5*...) while((s32[]{:T(128)}, f32[2048,4,64]{0,2,1:T(8,128)}, ...), condition=%wide.region_13.13_spmd.clone, body=%wide.region_11.12_spmd.clone.sunk | while | flops 2753165824 | bytes 243936352 | solution.py:164
  1579.1 35.8 %dynamic_update_slice.48 = f32[2,2048,4,64]{1,0,3,2:T(2,128)} dynamic-update-slice(f32[2,2048,4,64]{1,0,3,2:T(2,128)} %get-tuple-element.932, f32[1,2048,4,64]{1,0,3,2:T(1,128)S(1)} %copy.68, s32[]{:T(128)} %get-tuple-element.930, s32[]{:T(128)} %constant.249.clone.1..sunk.1, s32[]{:T(128)} %constant.249.clone.1..sunk.1, s32[]{:T(128)} %constant.249.clone.1..sunk.1) | dynamic-update-slice | bytes 4194308 | tf_op jit(solution)/shard_map/while/body/jit(dynamic_update_index_in_dim)/dynamic_update_slice | solution.py:169
  1676.7 21.2 convolution_convert_fusion.6
  1697.9 20.0 convolution_convert_fusion
  1718.0 25.0 %convolution_convert_fusion.1 = bf16[4096,2048]{1,0:T(8,128)(2,1)} fusion(bf16[4096,1024]{0,1:T(8,128)(2,1)} %get-tuple-element.527, bf16[1024,2048]{1,0:T(8,128)(2,1)} %param.28), kind=kOutput, calls=%fused_computation.69 | convolution fusion | flops 17188257792 | bytes 29360128 | tf_op jit(solution)/shard_map/dot_general | solution.py:228
  1763.2 153.0 %all-gather.15.cloned.1.call-done = bf16[8192,768]{1,0:T(8,128)(2,1)} async-done(((bf16[2048,768]{1,0:T(8,128)(2,1)}), bf16[8192,768]{1,0:T(8,128)(2,1)}) %all-gather.15.cloned.1.call-update) | async-done | bytes 12582928 | tf_op jit(solution)/shard_map/all_gather | solution.py:12
  1931.4 102.8 %reduce-scatter.11.cloned.1.call-done = bf16[512,2048]{1,0:T(8,128)(2,1)} async-done(((bf16[4096,2048]{1,0:T(8,128)(2,1)}), bf16[512,2048]{1,0:T(8,128)(2,1)}) %reduce-scatter.11.cloned.1.call-update) | async-done | bytes 2097168 | tf_op jit(solution)/shard_map/reduce_scatter | solution.py:286
  2037.1 39.5 %all-reduce = (f32[2048]{0:T(1024)S(1)}, f32[2048]{0:T(1024)S(1)}) all-reduce(f32[2048]{0:T(1024)S(1)} %get-tuple-element.446, f32[2048]{0:T(1024)S(1)} %copy-done.46), channel_id=1, replica_groups=mesh['dp'=4,'tensor'=8] {'dp','tensor'}, use_global_device_ids=true, to_apply=%region_18.19 | all-reduce | flops 4096 | bytes 32768 | tf_op jit(solution)/shard_map/psum | solution.py:302
  2077.9 76.1 %reduce-scatter.7.cloned.1.call-done = bf16[512,2048]{1,0:T(8,128)(2,1)} async-done(((bf16[4096,2048]{1,0:T(8,128)(2,1)}), bf16[512,2048]{1,0:T(8,128)(2,1)}) %reduce-scatter.7.cloned.1.call-update) | async-done | bytes 2097168 | tf_op jit(solution)/shard_map/reduce_scatter | solution.py:227
  (581 shorter events, 954.0 us)
Async XLA Ops:
  7.2 356.1 %copy-start = (bf16[256,2048]{1,0:T(8,128)(2,1)S(1)}, bf16[256,2048]{1,0:T(8,128)(2,1)}, u32[]{:S(2)}) copy-start(bf16[256,2048]{1,0:T(8,128)(2,1)} %param.24) | copy-start | bytes 3145732
  7.2 99.0 %all-gather.7.cloned.1.call-start = ((), (), s32[]{:S(2)}) async-start(), calls=%async_computation.4 | async-start | bytes 18874368 | tf_op jit(solution)/shard_map/all_gather | solution.py:210
  13.6 475.8 %reduce-scatter.5.cloned.1.call-start = ((), (), s32[]{:S(2)}) async-start(), calls=%async_computation.5 | async-start | bytes 18874368 | tf_op jit(solution)/shard_map/reduce_scatter | solution.py:215
  373.0 116.4 %copy-start.8 = (bf16[512,2048]{1,0:T(8,128)(2,1)S(1)}, bf16[512,2048]{1,0:T(8,128)(2,1)}, u32[]{:S(2)}) copy-start(bf16[512,2048]{1,0:T(8,128)(2,1)} %param.19) | copy-start | bytes 6291460
  373.1 119.4 %copy-start.36 = (f32[2048]{0:T(1024)S(1)}, f32[2048]{0:T(1024)}, u32[]{:S(2)}) copy-start(f32[2048]{0:T(1024)} %param.25) | copy-start | bytes 24580
  373.1 211.7 %all-gather.9.cloned.1.call-start = ((), (), s32[]{:S(2)}) async-start(), calls=%async_computation.6 | async-start | bytes 18874368 | tf_op jit(solution)/shard_map/all_gather | solution.py:223
  494.9 181.4 %all-gather.11.cloned.1.call-start = ((), (), s32[]{:S(2)}) async-start(), calls=%async_computation.8 | async-start | bytes 18874368 | tf_op jit(solution)/shard_map/all_gather | solution.py:235
  495.5 375.4 %reduce-scatter.9.cloned.1.call-start = ((), (), s32[]{:S(2)}) async-start(), calls=%async_computation.9 | async-start | bytes 18874368 | tf_op jit(solution)/shard_map/reduce_scatter | solution.py:251
  754.5 116.4 %copy-start.9 = (bf16[512,2048]{1,0:T(8,128)(2,1)S(1)}, bf16[512,2048]{1,0:T(8,128)(2,1)}, u32[]{:S(2)}) copy-start(bf16[512,2048]{1,0:T(8,128)(2,1)} %param.19) | copy-start | bytes 6291460
  754.5 116.4 %copy-start.37 = (f32[2048]{0:T(1024)S(1)}, f32[2048]{0:T(1024)}, u32[]{:S(2)}) copy-start(f32[2048]{0:T(1024)} %param.25) | copy-start | bytes 24580
  754.5 116.4 %copy-start.42 = (f32[512]{0:T(512)S(1)}, f32[512]{0:T(512)}, u32[]{:S(2)}) copy-start(f32[512]{0:T(512)} %copy-done.41) | copy-start | bytes 6148
  754.5 215.1 %all-gather.13.cloned.1.call-start = ((), (), s32[]{:S(2)}) async-start(), calls=%async_computation.10 | async-start | bytes 18874368 | tf_op jit(solution)/shard_map/all_gather | solution.py:264
  879.7 863.3 %all-reduce.4.cloned.1.call-start = ((), (), s32[]{:S(2)}) async-start(), calls=%async_computation.13 | async-start | bytes 27262976 | tf_op jit(solution)/shard_map/psum | solution.py:298
  997.5 918.6 %all-gather.15.cloned.1.call-start = ((), (), s32[]{:S(2)}) async-start(), calls=%async_computation.12 | async-start | bytes 15728640 | tf_op jit(solution)/shard_map/all_gather | solution.py:12
  1269.8 38.6 %copy-start.53 = (s32[2]{0:T(128)S(1)}, s32[2]{0:T(128)}, u32[]{:S(2)}) copy-start(s32[2]{0:T(128)} %copy-done.52) | copy-start | bytes 28 | tf_op jit(solution)/shard_map/while
  1697.9 336.3 %reduce-scatter.11.cloned.1.call-start = ((), (), s32[]{:S(2)}) async-start(), calls=%async_computation.11 | async-start | bytes 18874368 | tf_op jit(solution)/shard_map/reduce_scatter | solution.py:286
  1717.9 436.0 %reduce-scatter.7.cloned.1.call-start = ((), (), s32[]{:S(2)}) async-start(), calls=%async_computation.7 | async-start | bytes 18874368 | tf_op jit(solution)/shard_map/reduce_scatter | solution.py:227
  1925.1 109.0 %copy-start.10 = (bf16[512,2048]{1,0:T(8,128)(2,1)S(1)}, bf16[512,2048]{1,0:T(8,128)(2,1)}, u32[]{:S(2)}) copy-start(bf16[512,2048]{1,0:T(8,128)(2,1)} %param.19) | copy-start | bytes 6291460
  1925.1 109.0 %copy-start.39 = (f32[2048]{0:T(1024)S(1)}, f32[2048]{0:T(1024)}, u32[]{:S(2)}) copy-start(f32[2048]{0:T(1024)} %param.20) | copy-start | bytes 24580
  1925.1 109.0 %copy-start.45 = (f32[512]{0:T(512)S(1)}, f32[512]{0:T(512)}, u32[]{:S(2)}) copy-start(f32[512]{0:T(512)} %copy-done.44) | copy-start | bytes 6148
  1931.4 105.7 %copy-start.46 = (f32[2048]{0:T(1024)S(1)}, f32[2048]{0:T(1024)}, u32[]{:S(2)}) copy-start(f32[2048]{0:T(1024)} %get-tuple-element.444) | copy-start | bytes 24580
  1931.4 222.5 %copy-start.38 = (f32[2048]{0:T(1024)S(1)}, f32[2048]{0:T(1024)}, u32[]{:S(2)}) copy-start(f32[2048]{0:T(1024)} %param.25) | copy-start | bytes 24580
  1931.4 222.5 %copy-start.43 = (f32[512]{0:T(512)S(1)}, f32[512]{0:T(512)}, u32[]{:S(2)}) copy-start(f32[512]{0:T(512)} %copy-done.41) | copy-start | bytes 6148
  1931.4 222.5 %copy-start.48 = (f32[512]{0:T(512)S(1)}, f32[512]{0:T(512)}, u32[]{:S(2)}) copy-start(f32[512]{0:T(512)} %copy-done.47) | copy-start | bytes 6148
  (133 other events, 1354.1 us)
Sparse Core Ops, SparseCore 0:
  13.7 92.4 all-gather.6
  373.2 116.1 reduce-scatter.4
  495.0 89.7 all-gather.8
  586.5 89.7 all-gather.10
  754.6 116.1 reduce-scatter.8
  879.9 89.7 all-gather.12
  997.6 459.9 all-reduce.3
  1698.0 218.1 all-gather.14
  1919.7 114.3 reduce-scatter.10
  2037.6 116.3 reduce-scatter.6
